TPU v7x, 32 devices: a whole 2x2x4 slice. The times are simulated.
32 devices in a mesh: strip: 8 (over z, x), seq: 4 (over y, core).
Axes of the slice: x: 2, y: 2, z: 4, core: 2. Of those that a mesh axis runs over, the one named last changes fastest.
Arguments:
- patches: bfloat16 [32, 536, 768], P('strip', 'seq'), may hold values from -6 to 6
- lengths: int32 [32], P('strip'), may hold values from 1 to 536, as said below
- script: int32 [32], P('strip'), may hold values from 0 to 3, as said below
- script_table: bfloat16 [4, 768], replicated, may hold values from -3 to 3
- gain_one: float32 [768], replicated, may hold values from 0.25 to 1.75
- bias_one: float32 [768], replicated, may hold values from -2 to 2
- qkv_weight: bfloat16 [768, 2304], replicated, may hold values from -0.3125 to 0.3125
- query_bias: float32 [768], replicated, may hold values from -3 to 3
- value_bias: float32 [768], replicated, may hold values from -3 to 3
- out_weight: bfloat16 [768, 768], replicated, may hold values from -0.875 to 0.875
- out_bias: float32 [768], replicated, may hold values from -3 to 3
- gain_two: float32 [768], replicated, may hold values from 0.25 to 1.75
- bias_two: float32 [768], replicated, may hold values from -2 to 2
- up_weight: bfloat16 [768, 3072], replicated, may hold values from -0.21875 to 0.21875
- up_bias: float32 [3072], replicated, may hold values from -3 to 3
- down_weight: bfloat16 [3072, 768], replicated, may hold values from -0.109375 to 0.109375
- down_bias: float32 [768], replicated, may hold values from -3 to 3
- cotangent: bfloat16 [32, 536, 768], P('strip', 'seq'), may hold values from -6 to 6
Outputs:
- layer_out: bfloat16 [32, 536, 768], P('strip', 'seq')
- grad_patches: bfloat16 [32, 536, 768], P('strip', 'seq')
- grad_table: float32 [768, 4], P(('strip', 'seq'))
- grad_gain_one: float32 [768], P(('strip', 'seq'))
- grad_bias_one: float32 [768], P(('strip', 'seq'))
- grad_qkv: float32 [768, 2304], P(('strip', 'seq'))
- grad_query_bias: float32 [768], P(('strip', 'seq'))
- grad_value_bias: float32 [768], P(('strip', 'seq'))
- grad_out_weight: float32 [768, 768], P(('strip', 'seq'))
- grad_out_bias: float32 [768], P(('strip', 'seq'))
- grad_gain_two: float32 [768], P(('strip', 'seq'))
- grad_bias_two: float32 [768], P(('strip', 'seq'))
- grad_up_weight: float32 [768, 3072], P(('strip', 'seq'))
- grad_up_bias: float32 [3072], P(('strip', 'seq'))
- grad_down_weight: float32 [3072, 768], P(('strip', 'seq'))
- grad_down_bias: float32 [768], P(('strip', 'seq'))
Inputs may be any that keep to these rules, and one draw needn't show every extreme that they name: The first lengths[s] patch slots of strip s are filled; some strip has all 536 filled. `script`: script ids never fall from one strip to the next.
All inputs are finite; a program needn't handle non-finite values.
Results may differ from a plain program's by a relative error of at most 0.013.
The roundings to bfloat16 on the way count: a program that leaves them out, or rounds other values in their place, can miss the bound.
Values may be sent and summed in bfloat16 or wider, within the bound.
A program may use at most 192 MiB of HBM per device.

v0:
```python
import functools

import jax
import jax.numpy as jnp
from jax import lax
from jax.experimental import pallas as pl
from jax.experimental.pallas import tpu as pltpu
from jax.sharding import PartitionSpec as P

HD = 64


epsilon = 1e-12


def normalize(hidden):
    centred = hidden - jnp.mean(hidden, axis=-1, keepdims=True)
    inverse = lax.rsqrt(jnp.mean(centred * centred, axis=-1, keepdims=True) + epsilon)
    return (centred * inverse, inverse)


def norm_back(upstream, gain, normed, inverse):
    scaled = upstream * gain
    return inverse * (
        scaled
        - jnp.mean(scaled, axis=-1, keepdims=True)
        - normed * jnp.mean(scaled * normed, axis=-1, keepdims=True)
    )


def weight_grad(inputs, upstream):
    return lax.dot_general(
        inputs, upstream, (((0,), (0,)), ((), ())), preferred_element_type=jnp.float32
    )


def input_grad(upstream, weight):
    return lax.dot_general(
        upstream, weight, (((1,), (1,)), ((), ())), preferred_element_type=jnp.float32
    )


def gelu_slope(upper):
    return (
        0.5 * (1.0 + lax.erf(upper * 0.7071067811865476))
        + upper * jnp.exp(-0.5 * upper * upper) * 0.3989422804014327
    )


def split_block(block):
    seq_len = block.shape[0]
    heads_here = block.shape[2] // HD
    return [block[:, member].reshape(seq_len, heads_here, HD) for member in range(3)]


def masked_logits(queries, key_rows, length):
    logits = jnp.einsum(
        "qhd,khd->hqk", queries, key_rows, preferred_element_type=jnp.float32
    ) * HD ** (-0.5)
    visible = jnp.arange(logits.shape[-1], dtype=jnp.int32) < length
    return jnp.where(visible[None, None, :], logits, -1000000000.0)


def attend_forward(item):
    block, length = item
    queries, key_rows, values = split_block(block)
    logits = masked_logits(queries, key_rows, length)
    highest = jnp.max(logits, axis=-1, keepdims=True)
    expanded = jnp.exp(logits - highest)
    totals = jnp.sum(expanded, axis=-1, keepdims=True)
    probs = (expanded / totals).astype(jnp.bfloat16)
    mixed = jnp.einsum("hqk,khd->qhd", probs, values, preferred_element_type=jnp.float32)
    mixed = mixed.astype(jnp.bfloat16).reshape(block.shape[0], block.shape[2])
    return (mixed, (highest + jnp.log(totals))[..., 0])


def attend_backward(item):
    block, log_total, grad_mixed, length = item
    queries, key_rows, values = split_block(block)
    logits = masked_logits(queries, key_rows, length)
    probs = jnp.exp(logits - log_total[..., None])
    grad_heads = grad_mixed.reshape(queries.shape)
    grad_values = jnp.einsum(
        "hqk,qhd->khd", probs.astype(jnp.bfloat16), grad_heads, preferred_element_type=jnp.float32
    )
    grad_probs = jnp.einsum("qhd,khd->hqk", grad_heads, values, preferred_element_type=jnp.float32)
    inner = jnp.sum(probs * grad_probs, axis=-1, keepdims=True)
    grad_logits = (probs * (grad_probs - inner)).astype(jnp.bfloat16)
    grad_queries = jnp.einsum(
        "hqk,khd->qhd", grad_logits, key_rows, preferred_element_type=jnp.float32
    ) * HD ** (-0.5)
    grad_keys = jnp.einsum(
        "hqk,qhd->khd", grad_logits, queries, preferred_element_type=jnp.float32
    ) * HD ** (-0.5)
    stacked = jnp.stack([grad_queries, grad_keys, grad_values], axis=1)
    return stacked.reshape(block.shape).astype(jnp.bfloat16)


def local_general(
    patches,
    lengths,
    script,
    script_table,
    gain_one,
    bias_one,
    qkv_weight,
    query_bias,
    value_bias,
    out_weight,
    out_bias,
    gain_two,
    bias_two,
    up_weight,
    up_bias,
    down_weight,
    down_bias,
    cotangent,
):
    strips, row_count, model_width = patches.shape
    groups = script_table.shape[0]
    tokens = strips * row_count
    selector = (script[:, None] == jnp.arange(groups, dtype=jnp.int32)[None, :]).astype(jnp.float32)
    added = jnp.dot(selector.astype(jnp.bfloat16), script_table, preferred_element_type=jnp.float32)
    hidden = (patches.astype(jnp.float32) + added[:, None, :]).reshape(tokens, model_width)
    normed_one, inverse_one = normalize(hidden)
    inputs_one = (normed_one * gain_one + bias_one).astype(jnp.bfloat16)
    joint_bias = jnp.concatenate([query_bias, jnp.zeros_like(query_bias), value_bias])
    projected = (
        jnp.dot(inputs_one, qkv_weight, preferred_element_type=jnp.float32) + joint_bias
    ).astype(jnp.bfloat16)
    projected = projected.reshape(strips, row_count, 3, model_width)
    head_blocks = lax.all_to_all(projected, "seq", split_axis=3, concat_axis=1, tiled=True)
    mixed_heads, log_totals = lax.map(attend_forward, (head_blocks, lengths))
    mixed = lax.all_to_all(mixed_heads, "seq", split_axis=1, concat_axis=2, tiled=True).reshape(
        tokens, model_width
    )
    attended = hidden + jnp.dot(mixed, out_weight, preferred_element_type=jnp.float32) + out_bias
    normed_two, inverse_two = normalize(attended)
    inputs_two = (normed_two * gain_two + bias_two).astype(jnp.bfloat16)
    upper = jnp.dot(inputs_two, up_weight, preferred_element_type=jnp.float32) + up_bias
    active = jax.nn.gelu(upper, approximate=False).astype(jnp.bfloat16)
    result = attended + jnp.dot(active, down_weight, preferred_element_type=jnp.float32) + down_bias
    layer_out = result.astype(jnp.bfloat16).reshape(strips, row_count, model_width)
    grad_result = cotangent.reshape(tokens, model_width)
    grad_float = grad_result.astype(jnp.float32)
    grad_down_weight = weight_grad(active, grad_result)
    grad_down_bias = jnp.sum(grad_float, axis=0)
    grad_upper = (input_grad(grad_result, down_weight) * gelu_slope(upper)).astype(jnp.bfloat16)
    grad_up_weight = weight_grad(inputs_two, grad_upper)
    grad_up_bias = jnp.sum(grad_upper.astype(jnp.float32), axis=0)
    grad_inputs_two = input_grad(grad_upper, up_weight)
    grad_gain_two = jnp.sum(grad_inputs_two * normed_two, axis=0)
    grad_bias_two = jnp.sum(grad_inputs_two, axis=0)
    grad_attended = grad_float + norm_back(grad_inputs_two, gain_two, normed_two, inverse_two)
    grad_branch = grad_attended.astype(jnp.bfloat16)
    grad_out_weight = weight_grad(mixed, grad_branch)
    grad_out_bias = jnp.sum(grad_branch.astype(jnp.float32), axis=0)
    grad_mixed = (
        input_grad(grad_branch, out_weight)
        .astype(jnp.bfloat16)
        .reshape(strips, row_count, model_width)
    )
    grad_mixed_heads = lax.all_to_all(grad_mixed, "seq", split_axis=2, concat_axis=1, tiled=True)
    grad_heads = lax.map(attend_backward, (head_blocks, log_totals, grad_mixed_heads, lengths))
    grad_projected = lax.all_to_all(
        grad_heads, "seq", split_axis=1, concat_axis=3, tiled=True
    ).reshape(tokens, 3 * model_width)
    grad_qkv = weight_grad(inputs_one, grad_projected)
    grad_bias_rows = jnp.sum(grad_projected.astype(jnp.float32), axis=0)
    grad_query_bias = grad_bias_rows[:model_width]
    grad_value_bias = grad_bias_rows[2 * model_width :]
    grad_inputs_one = input_grad(grad_projected, qkv_weight)
    grad_gain_one = jnp.sum(grad_inputs_one * normed_one, axis=0)
    grad_bias_one = jnp.sum(grad_inputs_one, axis=0)
    grad_hidden = grad_attended + norm_back(grad_inputs_one, gain_one, normed_one, inverse_one)
    grad_patches = grad_hidden.astype(jnp.bfloat16).reshape(strips, row_count, model_width)
    per_strip = jnp.sum(grad_hidden.reshape(strips, row_count, model_width), axis=1)
    grad_table = jnp.dot(per_strip.T, selector, precision=lax.Precision.HIGHEST)
    summed = (
        lax.psum_scatter(grad_table, ("strip", "seq"), scatter_dimension=0, tiled=True),
        lax.psum_scatter(grad_gain_one, ("strip", "seq"), scatter_dimension=0, tiled=True),
        lax.psum_scatter(grad_bias_one, ("strip", "seq"), scatter_dimension=0, tiled=True),
        lax.psum_scatter(grad_qkv, ("strip", "seq"), scatter_dimension=0, tiled=True),
        lax.psum_scatter(grad_query_bias, ("strip", "seq"), scatter_dimension=0, tiled=True),
        lax.psum_scatter(grad_value_bias, ("strip", "seq"), scatter_dimension=0, tiled=True),
        lax.psum_scatter(grad_out_weight, ("strip", "seq"), scatter_dimension=0, tiled=True),
        lax.psum_scatter(grad_out_bias, ("strip", "seq"), scatter_dimension=0, tiled=True),
        lax.psum_scatter(grad_gain_two, ("strip", "seq"), scatter_dimension=0, tiled=True),
        lax.psum_scatter(grad_bias_two, ("strip", "seq"), scatter_dimension=0, tiled=True),
        lax.psum_scatter(grad_up_weight, ("strip", "seq"), scatter_dimension=0, tiled=True),
        lax.psum_scatter(grad_up_bias, ("strip", "seq"), scatter_dimension=0, tiled=True),
        lax.psum_scatter(grad_down_weight, ("strip", "seq"), scatter_dimension=0, tiled=True),
        lax.psum_scatter(grad_down_bias, ("strip", "seq"), scatter_dimension=0, tiled=True),
    )
    return (
        layer_out,
        grad_patches,
        summed[0],
        summed[1],
        summed[2],
        summed[3],
        summed[4],
        summed[5],
        summed[6],
        summed[7],
        summed[8],
        summed[9],
        summed[10],
        summed[11],
        summed[12],
        summed[13],
    )


MESH = pl.DeviceIdType.MESH
BF = jnp.bfloat16
F32 = jnp.float32
CHUNKS = 24
OWN = 16
SLOTS = 4
STAGES = 5
WIDE = 384
PART = 24
BLOCK = 32

PLAN = {
    "ffn": [
        [
            (0, 0, 0, 0, 0, 0, 0, 0, 0, 0, 0, 0, 0, 0, 0, 0, 0, 0, 0, 0),
            (0, 0, 0, 0, 0, 0, 0, 0, 0, 0, 2, 0, 0, 0, 0, 2, 0, 0, 0, 0),
            (2, 0, 0, 0, 0, 2, 0, 0, 0, 0, 4, 0, 0, 0, 0, 4, 0, 0, 0, 0),
            (4, 2, 0, 0, 0, 4, 1, 0, 0, 0, 6, 4, 0, 0, 0, 6, 3, 0, 0, 0),
        ],
        [
            (0, 0, 0, 0, 0, 0, 0, 0, 0, 0, 0, 0, 0, 0, 0, 0, 0, 0, 0, 0),
            (2, 0, 0, 0, 0, 2, 0, 0, 0, 0, 2, 0, 0, 0, 0, 2, 0, 0, 0, 0),
            (4, 0, 0, 0, 0, 4, 0, 0, 0, 0, 4, 2, 0, 0, 0, 4, 1, 0, 0, 0),
            (6, 4, 0, 0, 0, 6, 3, 0, 0, 0, 6, 4, 1, 0, 0, 6, 3, 0, 0, 0),
        ],
        [
            (0, 0, 0, 0, 0, 0, 0, 0, 0, 0, 0, 0, 0, 0, 0, 0, 0, 0, 0, 0),
            (2, 0, 0, 0, 0, 2, 0, 0, 0, 0, 2, 0, 0, 0, 0, 2, 0, 0, 0, 0),
            (4, 2, 0, 0, 0, 4, 1, 0, 0, 0, 4, 2, 0, 0, 0, 4, 1, 0, 0, 0),
            (6, 4, 1, 0, 0, 6, 3, 0, 0, 0, 6, 4, 1, 0, 0, 6, 4, 0, 0, 0),
        ],
    ],
    "after": [
        (6, 4, 1, 0, 0, 6, 4, 0, 0, 0, 8, 4, 3, 0, 0, 8, 4, 0, 0, 0),
        (8, 4, 3, 0, 0, 8, 4, 0, 0, 0, 8, 4, 3, 0, 0, 8, 4, 2, 0, 0),
        (8, 4, 3, 0, 0, 8, 4, 2, 0, 0, 8, 4, 4, 1, 0, 8, 4, 2, 0, 0),
    ],
    "pair": [
        (8, 4, 4, 1, 0, 8, 4, 2, 0, 0, 10, 4, 4, 1, 0, 8, 5, 3, 0, 0),
        (10, 4, 4, 1, 0, 8, 5, 3, 0, 0, 10, 6, 4, 1, 0, 8, 5, 3, 0, 0),
        (10, 6, 4, 1, 1, 8, 6, 3, 3, 0, 12, 8, 4, 1, 1, 8, 6, 3, 3, 0),
        (12, 8, 4, 1, 1, 8, 6, 3, 3, 0, 12, 8, 4, 3, 1, 8, 6, 5, 3, 2),
        (12, 10, 4, 4, 1, 8, 8, 5, 3, 3, 14, 10, 8, 4, 3, 8, 8, 6, 4, 3),
        (14, 10, 8, 4, 3, 8, 8, 6, 4, 3, 14, 12, 9, 4, 4, 8, 8, 6, 5, 3),
    ],
    "grad": [
        [
            (10, 6, 4, 1, 0, 8, 5, 3, 0, 0, 10, 6, 4, 1, 0, 8, 6, 3, 2, 0),
            (12, 8, 4, 3, 1, 8, 6, 5, 3, 2, 12, 8, 4, 4, 1, 8, 8, 5, 3, 3),
            (14, 12, 9, 4, 4, 8, 8, 6, 5, 3, 14, 12, 9, 6, 4, 8, 8, 8, 5, 3),
        ],
        [
            (10, 6, 4, 1, 0, 8, 6, 3, 2, 0, 10, 6, 4, 1, 1, 8, 6, 3, 3, 0),
            (12, 8, 4, 4, 1, 8, 8, 5, 3, 3, 12, 10, 4, 4, 1, 8, 8, 5, 3, 3),
            (14, 12, 9, 6, 4, 8, 8, 8, 5, 3, 14, 12, 10, 8, 4, 8, 8, 8, 5, 4),
        ],
    ],
    "last": [
        (14, 12, 10, 8, 4, 8, 8, 8, 5, 4, 16, 13, 11, 8, 4, 8, 8, 8, 6, 4),
        (16, 13, 11, 8, 4, 8, 8, 8, 6, 4, 16, 14, 11, 8, 4, 8, 8, 8, 6, 4),
    ],
    "tail": [
        (16, 14, 11, 8, 4, 8, 8, 8, 6, 4, 16, 14, 12, 8, 4, 8, 8, 8, 6, 4),
        (16, 14, 12, 8, 4, 8, 8, 8, 6, 4, 16, 14, 12, 10, 4, 8, 8, 8, 6, 4),
        (16, 14, 12, 10, 4, 8, 8, 8, 6, 4, 16, 14, 12, 10, 4, 8, 8, 8, 6, 5),
        (16, 14, 12, 10, 4, 8, 8, 8, 6, 5, 16, 14, 12, 10, 5, 8, 8, 8, 6, 5),
        (16, 14, 12, 10, 5, 8, 8, 8, 6, 5, 16, 14, 12, 10, 6, 8, 8, 8, 6, 5),
        (16, 14, 12, 10, 6, 8, 8, 8, 6, 5, 16, 14, 12, 10, 6, 8, 8, 8, 7, 5),
        (16, 14, 12, 10, 6, 8, 8, 8, 7, 5, 16, 14, 13, 10, 6, 8, 8, 8, 7, 5),
        (16, 14, 13, 10, 6, 8, 8, 8, 7, 5, 16, 14, 13, 10, 6, 8, 8, 8, 8, 5),
        (16, 14, 13, 10, 6, 8, 8, 8, 8, 5, 16, 14, 13, 10, 7, 8, 8, 8, 8, 5),
        (16, 14, 13, 10, 7, 8, 8, 8, 8, 5, 16, 14, 13, 10, 8, 8, 8, 8, 8, 5),
        (16, 14, 13, 10, 8, 8, 8, 8, 8, 5, 16, 15, 13, 10, 8, 8, 8, 8, 8, 5),
        (16, 15, 13, 10, 8, 8, 8, 8, 8, 5, 16, 15, 13, 11, 8, 8, 8, 8, 8, 5),
        (16, 15, 13, 11, 8, 8, 8, 8, 8, 5, 16, 15, 13, 11, 8, 8, 8, 8, 8, 6),
        (16, 15, 13, 11, 8, 8, 8, 8, 8, 6, 16, 15, 14, 11, 8, 8, 8, 8, 8, 6),
        (16, 15, 14, 11, 8, 8, 8, 8, 8, 6, 16, 16, 14, 11, 8, 8, 8, 8, 8, 6),
        (16, 16, 14, 11, 8, 8, 8, 8, 8, 6, 16, 16, 14, 11, 9, 8, 8, 8, 8, 6),
        (16, 16, 14, 11, 9, 8, 8, 8, 8, 6, 16, 16, 14, 11, 10, 8, 8, 8, 8, 6),
        (16, 16, 14, 11, 10, 8, 8, 8, 8, 6, 16, 16, 14, 13, 10, 8, 8, 8, 8, 6),
        (16, 16, 14, 13, 10, 8, 8, 8, 8, 6, 16, 16, 14, 13, 10, 8, 8, 8, 8, 7),
        (16, 16, 14, 13, 10, 8, 8, 8, 8, 7, 16, 16, 15, 13, 10, 8, 8, 8, 8, 7),
        (16, 16, 15, 13, 10, 8, 8, 8, 8, 7, 16, 16, 15, 14, 11, 8, 8, 8, 8, 7),
        (16, 16, 15, 14, 11, 8, 8, 8, 8, 7, 16, 16, 16, 14, 11, 8, 8, 8, 8, 8),
        (16, 16, 16, 14, 11, 8, 8, 8, 8, 8, 16, 16, 16, 14, 12, 8, 8, 8, 8, 8),
        (16, 16, 16, 14, 12, 8, 8, 8, 8, 8, 16, 16, 16, 14, 13, 8, 8, 8, 8, 8),
        (16, 16, 16, 14, 13, 8, 8, 8, 8, 8, 16, 16, 16, 15, 13, 8, 8, 8, 8, 8),
        (16, 16, 16, 15, 13, 8, 8, 8, 8, 8, 16, 16, 16, 16, 13, 8, 8, 8, 8, 8),
        (16, 16, 16, 16, 13, 8, 8, 8, 8, 8, 16, 16, 16, 16, 14, 8, 8, 8, 8, 8),
        (16, 16, 16, 16, 14, 8, 8, 8, 8, 8, 16, 16, 16, 16, 15, 8, 8, 8, 8, 8),
        (16, 16, 16, 16, 15, 8, 8, 8, 8, 8, 16, 16, 16, 16, 16, 8, 8, 8, 8, 8),
    ],
}


def fits(mesh):
    return dict(mesh.shape) == {"strip": 8, "seq": 4}


def dot(left, right, left_dim, right_dim):
    return lax.dot_general(
        left, right, (((left_dim,), (right_dim,)), ((), ())), preferred_element_type=F32
    )


def mean(block):
    return jnp.mean(block, axis=1, keepdims=True)


def fold(block):
    return jnp.sum(block.reshape(block.shape[0] // 8, 8, block.shape[1]), axis=0)


def sweep(blocks, body, totals):
    def trip(first, size, totals):
        results = [body(first + k) for k in range(size)]
        for stores, _ in results:
            for ref, at, value in stores:
                ref[at] = value
        return tuple(
            total + sum(sums[k] for _, sums in results) for k, total in enumerate(totals)
        )

    totals = lax.fori_loop(0, blocks // 4, lambda i, t: trip(4 * i, 4, t), totals)
    if blocks % 4:
        totals = trip(blocks // 4 * 4, blocks % 4, totals)
    return totals


def block_rows(b):
    if isinstance(b, int):
        return pl.ds(b * BLOCK, BLOCK)
    return pl.ds(pl.multiple_of(b * BLOCK, BLOCK), BLOCK)


def column_sum(block):
    return jnp.sum(block, axis=0, keepdims=True)


def attend_pair(pair, length, proj, mixed, lse_all):
    count = proj.shape[0]
    width = proj.shape[1] // 3
    at = lambda part: pl.ds(pl.multiple_of(part * width + pair * 128, 128), 128)
    lane = lax.broadcasted_iota(jnp.int32, (1, 128), 1)
    visible = lax.broadcasted_iota(jnp.int32, (1, count), 1) < length
    q = proj[:, at(0)] * jnp.asarray(0.125, BF)
    k = proj[:, at(1)]
    v = proj[:, at(2)]
    outs, logs = [], []
    for head in range(2):
        own = (lane // HD) == head
        logits = dot(jnp.where(own, q, jnp.zeros_like(q)), k, 1, 1)
        logits = jnp.where(visible, logits, -1000000000.0)
        highest = jnp.max(logits, axis=1, keepdims=True)
        expanded = jnp.exp(logits - highest)
        total = jnp.sum(expanded, axis=1, keepdims=True)
        probs = (expanded * (1.0 / total)).astype(BF)
        outs.append(dot(probs, v, 1, 0))
        logs.append(highest + jnp.log(total))
    mixed[:, at(0)] = jnp.where(lane < HD, outs[0], outs[1]).astype(BF)
    known = jnp.where(lane == 2 * pair, logs[0], lse_all[...])
    lse_all[...] = jnp.where(lane == 2 * pair + 1, logs[1], known)


def attend_pair_back(pair, length, proj, gmixed, lse_all):
    count = proj.shape[0]
    width = proj.shape[1] // 3
    at = lambda part: pl.ds(pl.multiple_of(part * width + pair * 128, 128), 128)
    lane = lax.broadcasted_iota(jnp.int32, (1, 128), 1)
    visible = lax.broadcasted_iota(jnp.int32, (1, count), 1) < length
    q = proj[:, at(0)] * jnp.asarray(0.125, BF)
    k = proj[:, at(1)]
    v = proj[:, at(2)]
    gm = gmixed[:, at(0)]
    lse = lse_all[...]
    grads = []
    for head in range(2):
        own = (lane // HD) == head
        q_own = jnp.where(own, q, jnp.zeros_like(q))
        g_own = jnp.where(own, gm, jnp.zeros_like(gm))
        k_own = jnp.where(own, k, jnp.zeros_like(k))
        own_lse = jnp.sum(jnp.where(lane == 2 * pair + head, lse, 0.0), axis=1, keepdims=True)
        logits = dot(q_own, k, 1, 1)
        probs = jnp.where(visible, jnp.exp(logits - own_lse), 0.0)
        grad_probs = dot(g_own, v, 1, 1)
        inner = jnp.sum(probs * grad_probs, axis=1, keepdims=True)
        grad_logits = (probs * (grad_probs - inner)).astype(BF)
        grads.append(
            (
                dot(grad_logits, k_own, 1, 0),
                dot(q_own, grad_logits, 0, 0),
                dot(g_own, probs.astype(BF), 0, 0),
            )
        )
    gq = ((grads[0][0] + grads[1][0]) * 0.125).astype(BF)
    gk = (grads[0][1] + grads[1][1]).T.astype(BF)
    gv = (grads[0][2] + grads[1][2]).T.astype(BF)
    return gq, gk, gv


class Devices:
    def __init__(self):
        s, q = lax.axis_index("strip"), lax.axis_index("seq")
        self.s, self.q = s, q
        self.core, self.y = q % 2, q // 2
        self.x, self.low, self.high = s % 2, (s // 2) % 2, s // 4
        self.to_core = (s, q + 1 - 2 * self.core)
        self.to_y = (s, q + 2 - 4 * self.y)
        self.to_x = (s + 1 - 2 * self.x, q)
        self.to_low = (s + 2 - 4 * self.low, q)
        self.to_high = (s + 4 - 8 * self.high, q)
        self.to_far = (s + 2 - 4 * self.low + 4 - 8 * self.high, q)


def pick(index, values):
    chosen = values[0]
    for position in range(1, len(values)):
        change = values[position] - values[position - 1]
        if change:
            chosen = chosen + jnp.where(index >= position, change, 0)
    return chosen


class Reduction:
    def __init__(self, dev, g, r1, r2, r3, r4, s4, r5, r4d, r5d, write, write_down, send, recv):
        self.dev = dev
        self.bufs = (g, r1, r2, r3, r4, s4, r5, r4d, r5d)
        self.write = write
        self.write_down = write_down
        self.sems = (send, recv)

    def side(self, stage, c, down):
        dev = self.dev
        odd = c % 2
        even = 1 - odd
        if down:
            by_x, by_y, by_low = ((odd, even, 0), (even, odd, 0), (0, 0, 1))[stage - 1]
        else:
            by_x, by_y, by_low = ((even, 0, odd), (odd, even, 0), (0, odd, even))[stage - 1]
        device = (
            dev.s + by_x * (1 - 2 * dev.x) + by_low * (2 - 4 * dev.low),
            dev.q + by_y * (2 - 4 * dev.y),
        )
        return device, by_x * dev.x + by_y * dev.y + by_low * dev.low

    def slot(self, c, down):
        return c % SLOTS + SLOTS if down else c % SLOTS

    def copy(self, stage, c, down):
        g, r1, r2, r3, r4, s4, r5, r4d, r5d = self.bufs
        dev = self.dev
        if stage == 0:
            source, target = g.at[self.slot(c, down), 1 - dev.core], r1.at[c]
            device = dev.to_core
        elif stage == 4:
            device = dev.to_high
            if down:
                source, target = r4d.at[c - OWN], r5d.at[c - OWN]
            else:
                source, target = s4.at[c, 1 - dev.high], r5.at[c]
        elif stage == 3 and down:
            source, target, device = r3.at[c], r4d.at[c - OWN], dev.to_low
        else:
            device, bit = self.side(stage, c, down)
            rows = 384 >> stage
            held, target = ((r1, r2), (r2, r3), (r3, r4))[stage - 1]
            source, target = held.at[c, pl.ds((1 - bit) * rows, rows)], target.at[c]
        send, recv = self.sems
        return pltpu.make_async_remote_copy(
            src_ref=source,
            dst_ref=target,
            send_sem=send.at[stage, c],
            recv_sem=recv.at[stage, c],
            device_id=device,
            device_id_type=MESH,
        )

    def near(self, c):
        return self.dev.low == (c - OWN) // 2 % 2

    def far(self, c):
        return self.dev.high == (c - OWN) // 4

    def free(self, c, down):
        first = OWN if down else 0

        @pl.when(c >= first + SLOTS)
        def _():
            self.copy(0, c - SLOTS, down).wait_send()

    def start(self, c, down):
        self.copy(0, c, down).start()

    def event(self, stage, c, down):
        g, r1, r2, r3, r4, s4, r5, r4d, r5d = self.bufs
        dev = self.dev
        if stage >= 3 and down:
            self.last_events(stage, c)
            return
        self.copy(stage, c, down).wait_recv()
        if stage == 0:
            slot = self.slot(c, down)

            @pl.loop(0, 4)
            def _(i):
                rows = pl.ds(i * 96, 96)
                r1[c, rows] = r1[c, rows] + g[slot, dev.core, rows]
        elif stage < 3:
            _, bit = self.side(stage, c, down)
            held, target = ((r1, r2), (r2, r3))[stage - 1]

            @pl.loop(0, 4 >> stage)
            def _(i):
                rows = pl.ds(i * 96, 96)
                kept = pl.ds(pl.multiple_of(bit * (384 >> stage) + i * 96, 96), 96)
                target[c, rows] = target[c, rows] + held[c, kept]
        elif stage == 3:
            _, bit = self.side(stage, c, down)
            kept = pl.ds(pl.multiple_of(bit * 48, 48), 48)
            total = r4[c].astype(F32) + r3[c, kept].astype(F32)
            s4[c, 0] = total[:24].astype(BF)
            s4[c, 1] = total[24:].astype(BF)
        else:
            self.write[c] = s4[c, dev.high].astype(F32) + r5[c].astype(F32)
            return
        if stage == 2 and down:

            @pl.when(jnp.logical_not(self.near(c)))
            def _():
                self.copy(3, c, down).start()
        else:
            self.copy(stage + 1, c, down).start()

    def last_events(self, stage, c):
        r3, r4d, r5d = self.bufs[3], self.bufs[7], self.bufs[8]

        @pl.when(self.near(c))
        def _():
            if stage == 3:
                self.copy(3, c, True).wait_recv()
                r4d[c - OWN] = r4d[c - OWN] + r3[c]

                @pl.when(jnp.logical_not(self.far(c)))
                def _():
                    self.copy(4, c, True).start()
            else:

                @pl.when(self.far(c))
                def _():
                    self.copy(4, c, True).wait_recv()
                    total = r4d[c - OWN].astype(F32) + r5d[c - OWN].astype(F32)
                    self.write_down[c % 2] = total

    def step(self, plans, index=0):
        for column in (4, 9, 3, 8, 2, 7, 1, 6, 0, 5):
            low = pick(index, [plan[column] for plan in plans])
            high = pick(index, [plan[2 * STAGES + column] for plan in plans])
            if all(plan[column] == plan[2 * STAGES + column] for plan in plans):
                continue
            down = column >= STAGES
            first = OWN if down else 0

            @pl.loop(low + first, high + first)
            def _(c):
                self.event(column % STAGES, c, down)

    def finish(self):
        for down in (False, True):
            first, last = (OWN, CHUNKS) if down else (0, OWN)

            @pl.loop(last - SLOTS, last)
            def _(c):
                self.copy(0, c, down).wait_send()

            @pl.loop(first, last)
            def _(c):
                for stage in range(1, STAGES):
                    if down and stage == 3:

                        @pl.when(jnp.logical_not(self.near(c)))
                        def _():
                            self.copy(3, c, True).wait_send()
                    elif down and stage == 4:

                        @pl.when(self.near(c) & jnp.logical_not(self.far(c)))
                        def _():
                            self.copy(4, c, True).wait_send()
                    else:
                        self.copy(stage, c, down).wait_send()

    def place(self, c, half, product):
        columns = pl.ds(half * WIDE, WIDE)
        for owner in range(32):
            core, y, x, low, high = [(owner >> bit) % 2 for bit in range(5)]
            unit = 4 * low + 2 * x + y if half else 4 * x + 2 * y + low
            self.bufs[0][self.slot(c, False), core, pl.ds(unit * 48 + high * PART, PART)] = product[
                pl.ds(owner * PART, PART), columns
            ]

    def place_down(self, c, half, product):
        columns = pl.ds(half * WIDE, WIDE)
        for owner in range(8):
            core, y, x = [(owner >> bit) % 2 for bit in range(3)]
            unit = 2 * x + y if half else 2 * y + x
            self.bufs[0][self.slot(c, True), core, pl.ds(unit * 96, 96)] = product[
                pl.ds(owner * 96, 96), columns
            ]


ERF_TOP = (
    0.00022905065861350646, 0.0034082910107109506, 0.050955695062380861, 0.18520832239976145,
    1.128379143519084,
)
ERF_BOTTOM = (
    -1.1791602954361697e-7, 0.000023547966471313185, 0.0010179625278914885,
    0.014070470171167667, 0.11098505178285362, 0.49746925110067538, 1.0,
)


def erf(value):
    value = jnp.clip(value, -3.832506856900711, 3.832506856900711)
    square = value * value
    top = jnp.full_like(square, ERF_TOP[0])
    for term in ERF_TOP[1:]:
        top = top * square + term
    bottom = jnp.full_like(square, ERF_BOTTOM[0])
    for term in ERF_BOTTOM[1:]:
        bottom = bottom * square + term
    return value * top / bottom


def standardize(block):
    centred = block - mean(block)
    inverse = lax.rsqrt(mean(centred * centred) + epsilon)
    return centred * inverse, inverse


def layer_kernel(
    lengths, script, table, gain_one, bias_one, query_bias, value_bias, out_bias, gain_two,
    bias_two, up_bias, down_bias, patches, cotangent, qkv_hbm, out_hbm, up_hbm, down_hbm,
    layer_out, grad_patches, reduced, reduced_down, small,
    outgoing, xin, cin, hidden, n1, proj, mixed, lse_all, att, n2, cot, res, gn, branch, gmixed,
    gblk, act, product, jbias, ubias, early, late, wqkv, wout, wup, wdown,
    g, r1, r2, r3, r4, s4, r5, r4d, r5d, early_in, late_in,
    send, recv, vsend, vrecv, xsend, xrecv, wsem, fsem, osem,
):
    row_count, strips, width = patches.shape
    count = strips * row_count
    rows = hidden.shape[0]
    blocks = rows // BLOCK
    ff_blocks = up_hbm.shape[1] // width
    dev = Devices()
    s, q = dev.s, dev.q
    red = Reduction(
        dev, g, r1, r2, r3, r4, s4, r5, r4d, r5d, reduced, reduced_down, send, recv
    )

    barrier = pltpu.get_barrier_semaphore()
    greeted = [(s, (q + hop) % strips) for hop in range(1, strips)]
    greeted += [dev.to_x, dev.to_low, dev.to_high, dev.to_far]
    for device in greeted:
        pl.semaphore_signal(barrier, inc=1, device_id=device, device_id_type=MESH)

    load_qkv = pltpu.make_async_copy(qkv_hbm, wqkv, wsem.at[0])
    load_out = pltpu.make_async_copy(out_hbm, wout, wsem.at[1])

    def load_ff(block):
        columns = pl.ds(pl.multiple_of(block * width, width), width)
        slot = block % 2
        return (
            pltpu.make_async_copy(up_hbm.at[:, columns], wup.at[slot], fsem.at[0, slot]),
            pltpu.make_async_copy(down_hbm.at[columns], wdown.at[slot], fsem.at[1, slot]),
        )

    def exchange(group, source, target):
        copies = []
        for hop in range(1, strips):
            other = (q + hop) % strips
            copies.append(
                pltpu.make_async_remote_copy(
                    src_ref=source.at[other],
                    dst_ref=target.at[q],
                    send_sem=xsend.at[group, hop],
                    recv_sem=xrecv.at[group, hop],
                    device_id=(s, other),
                    device_id_type=MESH,
                )
            )
        own = pltpu.make_async_copy(source.at[q], target.at[q], osem.at[group])
        return copies, own

    def launch(moves):
        copies, own = moves
        for index in (1, 0, 2):
            copies[index].start()
        own.start()

    def arrive(moves):
        copies, own = moves
        for copy in copies:
            copy.wait_recv()
        own.wait()

    def share(group, total, arrived):
        steps = [
            [(s, (q + hop) % strips) for hop in range(1, strips)],
            [dev.to_x],
            [dev.to_low, dev.to_high, dev.to_far],
        ]

        def copies(step):
            first = (0, 3, 4)[step]
            return [
                pltpu.make_async_remote_copy(
                    src_ref=total,
                    dst_ref=arrived.at[first + k],
                    send_sem=vsend.at[group, first + k],
                    recv_sem=vrecv.at[group, first + k],
                    device_id=device,
                    device_id_type=MESH,
                )
                for k, device in enumerate(steps[step])
            ]

        def begin(step):
            for copy in copies(step):
                copy.start()

        def end(step):
            first = (0, 3, 4)[step]
            moves = copies(step)
            for copy in moves:
                copy.wait_recv()
            for copy in moves:
                copy.wait_send()
            total[...] = total[...] + sum(arrived[first + k] for k in range(len(moves)))
            if step < 2:
                begin(step + 1)

        return begin, end

    def sent(moves):
        for copy in moves[0]:
            copy.wait_send()
        return moves

    into_x = exchange(0, outgoing, xin)
    into_c = exchange(1, outgoing, cin)
    for j in range(strips):
        outgoing[j] = patches[:, j, :]
    pl.semaphore_wait(barrier, len(greeted))
    launch(into_x)
    load_qkv.start()
    load_out.start()
    for copy in load_ff(0):
        copy.start()

    length = lengths[q]
    own_script = script[q]
    added = jnp.zeros((1, width), F32)
    for group in range(table.shape[0]):
        added = jnp.where(own_script == group, table[pl.ds(group, 1)].astype(F32), added)
    row = lambda ref: ref[...].reshape(1, ref.shape[0])
    jbias[pl.ds(0, 1)] = row(query_bias)
    jbias[pl.ds(1, 1)] = jnp.zeros((1, width), F32)
    jbias[pl.ds(2, 1)] = row(value_bias)
    hidden[pl.ds(count, rows - count)] = jnp.zeros((rows - count, width), F32)
    gn[pl.ds(count, rows - count)] = jnp.zeros((rows - count, width), F32)
    lse_all[...] = jnp.zeros_like(lse_all)

    for block in range(ff_blocks):
        ubias[pl.ds(block, 1)] = row(up_bias)[:, block * width : block * width + width]

    arrive(into_x)
    sent(into_x)
    for j in range(strips):
        outgoing[j] = cotangent[:, j, :]
    launch(into_c)
    for j in range(strips):
        hidden[pl.ds(j * row_count, row_count)] = xin[j].astype(F32) + added

    def first_norm(b):
        at = block_rows(b)
        normed, _ = standardize(hidden[at])
        return [(n1, at, (normed * row(gain_one) + row(bias_one)).astype(BF))], ()

    sweep(blocks, first_norm, ())

    load_qkv.wait()

    @pl.loop(0, 3)
    def _(part):
        columns = pl.ds(pl.multiple_of(part * width, width), width)
        proj[:, columns] = (dot(n1[...], wqkv[:, columns], 1, 0) + jbias[pl.ds(part, 1)]).astype(BF)

    @pl.loop(0, width // 128)
    def _(pair):
        attend_pair(pair, length, proj, mixed, lse_all)

    arrive(into_c)
    for j in range(strips):
        gn[pl.ds(j * row_count, row_count)] = cin[j].astype(F32)
    load_out.wait()
    att[...] = hidden[...] + dot(mixed[...], wout[...], 1, 0) + row(out_bias)
    zero8 = jnp.zeros((8, width), F32)

    def second_norm(b):
        at = block_rows(b)
        block = att[at]
        normed, _ = standardize(block)
        upstream = gn[at]
        stores = [
            (n2, at, (normed * row(gain_two) + row(bias_two)).astype(BF)),
            (res, at, block + row(down_bias)),
            (cot, at, upstream.astype(BF)),
            (gn, at, jnp.zeros((BLOCK, width), F32)),
        ]
        return stores, (fold(upstream),)

    early[pl.ds(3, 1)] = column_sum(sweep(blocks, second_norm, (zero8,))[0])

    @pl.loop(0, ff_blocks)
    def _(block):
        slot = block % 2
        for copy in load_ff(block):
            copy.wait()

        @pl.when(block + 1 < ff_blocks)
        def _():
            for copy in load_ff(block + 1):
                copy.start()

        up = wup[slot]
        down = wdown[slot]
        upper = dot(n2[...], up, 1, 0) + ubias[pl.ds(block, 1)]
        grad_active = dot(cot[...], down, 1, 1)
        share = 0.5 * (1.0 + erf(upper * 0.7071067811865476))
        act[...] = (upper * share).astype(BF)
        slope = share + upper * jnp.exp(-0.5 * upper * upper) * 0.3989422804014327
        grad_upper = (grad_active * slope).astype(BF)
        gblk[...] = grad_upper
        res[...] += dot(act[...], down, 1, 0)
        gn[...] += dot(grad_upper, up, 1, 1)
        early[pl.ds(4 + block, 1)] = column_sum(grad_upper.astype(F32))
        red.step(PLAN["ffn"][0], block)
        product[...] = dot(n2[...], gblk[...], 0, 0).astype(BF)
        for half in range(2):
            c = 2 * block + half
            red.free(c, False)
            red.place(c, half, product)
            red.start(c, False)
        red.step(PLAN["ffn"][1], block)
        product[...] = dot(act[...], cot[...], 0, 0).astype(BF)
        for half in range(2):
            c = OWN + 2 * block + half
            red.free(c, True)
            red.place_down(c, half, product)
            red.start(c, True)
        red.step(PLAN["ffn"][2], block)

    sent(into_c)
    for j in range(strips):
        outgoing[j] = res[pl.ds(j * row_count, row_count)].astype(BF)
    from_out = exchange(2, outgoing, layer_out)
    launch(from_out)

    def second_back(b):
        at = block_rows(b)
        normed, inverse = standardize(att[at])
        upstream = gn[at]
        scaled = upstream * row(gain_two)
        back = inverse * (scaled - mean(scaled) - normed * mean(scaled * normed))
        grad = cot[at].astype(F32) + back
        rounded = grad.astype(BF)
        sums = (fold(upstream * normed), fold(upstream), fold(rounded.astype(F32)))
        return [(gn, at, grad), (branch, at, rounded)], sums

    totals = sweep(blocks, second_back, (zero8, zero8, zero8))
    early[pl.ds(0, 1)] = column_sum(totals[0])
    early[pl.ds(1, 1)] = column_sum(totals[1])
    early[pl.ds(2, 1)] = column_sum(totals[2])
    share_early = share(0, early, early_in)
    share_early[0](0)
    red.step(PLAN["after"][:1])
    gmixed[...] = dot(branch[...], wout[...], 1, 1).astype(BF)
    red.step(PLAN["after"][1:2])
    product[...] = dot(mixed[...], branch[...], 0, 0).astype(BF)
    for half in range(2):
        c = 8 + half
        red.free(c, False)
        red.place(c, half, product)
        red.start(c, False)
    red.step(PLAN["after"][2:])

    res[...] = jnp.zeros_like(res)

    @pl.loop(0, 3)
    def _(i):
        @pl.loop(0, 2)
        def _(h):
            pair = 2 * i + h
            grads = attend_pair_back(pair, length, proj, gmixed, lse_all)
            for part in range(3):
                gblk[:, pl.ds(pl.multiple_of(h * WIDE + part * 128, 128), 128)] = grads[part]
            lanes = pl.ds(pl.multiple_of(pair * 128, 128), 128)
            late[pl.ds(2, 1), lanes] = column_sum(grads[0].astype(F32))
            late[pl.ds(3, 1), lanes] = column_sum(grads[2].astype(F32))
            red.step(PLAN["pair"], pair)

        product[...] = dot(n1[...], gblk[...], 0, 0).astype(BF)
        for half in range(2):
            c = 10 + 2 * i + half
            red.free(c, False)
            red.place(c, half, product)
            red.start(c, False)
        red.step(PLAN["grad"][0], i)
        weights = jnp.concatenate(
            [
                wqkv[:, pl.ds(pl.multiple_of(part * width + (2 * i + h) * 128, 128), 128)]
                for h in range(2)
                for part in range(3)
            ],
            axis=1,
        )
        res[...] += dot(gblk[...], weights, 1, 1)
        red.step(PLAN["grad"][1], i)
        for turn in range(3):

            @pl.when(i == turn)
            def _():
                share_early[1](turn)

    def first_back(b):
        at = block_rows(b)
        normed, inverse = standardize(hidden[at])
        upstream = res[at]
        scaled = upstream * row(gain_one)
        back = inverse * (scaled - mean(scaled) - normed * mean(scaled * normed))
        grad = gn[at] + back
        return [(res, at, grad)], (fold(upstream * normed), fold(upstream), fold(grad))

    totals = sweep(blocks, first_back, (zero8, zero8, zero8))
    red.step(PLAN["last"][:1])
    late[pl.ds(0, 1)] = column_sum(totals[0])
    late[pl.ds(1, 1)] = column_sum(totals[1])
    strip_sum = column_sum(totals[2])
    for group in range(table.shape[0]):
        late[pl.ds(4 + group, 1)] = jnp.where(own_script == group, strip_sum, 0.0)
    share_late = share(1, late, late_in)
    share_late[0](0)
    for j in range(strips):
        xin[j] = res[pl.ds(j * row_count, row_count)].astype(BF)
    from_grad = exchange(3, xin, grad_patches)
    launch(from_grad)
    red.step(PLAN["last"][1:])
    tail = PLAN["tail"]
    turns = [len(tail) * (turn + 1) // 4 for turn in range(3)]
    for index in range(len(tail)):
        red.step(tail[index : index + 1])
        for turn in range(3):
            if turns[turn] == index:
                share_late[1](turn)

    owner = s * strips + q
    spread = lax.broadcasted_iota(jnp.int32, (width, 128), 0)
    lane = lax.broadcasted_iota(jnp.int32, (width, 128), 1)
    few = jnp.where((spread == PART * owner + lane) & (lane < PART), 1.0, 0.0)
    many = jnp.where((spread == 4 * PART * (owner % 8) + lane) & (lane < 4 * PART), 1.0, 0.0)
    exact = lambda left, right: lax.dot_general(
        left, right, (((1,), (0,)), ((), ())), precision=lax.Precision.HIGHEST,
        preferred_element_type=F32,
    )
    lines = lax.broadcasted_iota(jnp.int32, (8, width), 0)
    chosen = jnp.where(lines == 4 + owner // 8, early[...], 0.0)
    small[pl.ds(0, 8)] = exact(early[...], few)
    small[pl.ds(8, 8)] = exact(late[...], few)
    small[pl.ds(16, 8)] = exact(chosen, many)

    red.finish()
    for moves in (from_out, from_grad):
        arrive(moves)
        sent(moves)


def run_layer(*arrays):
    patches = arrays[12]
    row_count, strips, width = patches.shape
    rows = -(-strips * row_count // BLOCK) * BLOCK
    vmem = pl.BlockSpec(memory_space=pltpu.VMEM)
    smem = pl.BlockSpec(memory_space=pltpu.SMEM)
    hbm = pl.BlockSpec(memory_space=pl.ANY)
    packed = lambda *shape: pltpu.VMEM(shape, BF)
    wide = lambda *shape: pltpu.VMEM(shape, F32)
    return pl.pallas_call(
        layer_kernel,
        out_shape=[
            jax.ShapeDtypeStruct((strips, row_count, width), BF),
            jax.ShapeDtypeStruct((strips, row_count, width), BF),
            jax.ShapeDtypeStruct((OWN, PART, WIDE), F32),
            jax.ShapeDtypeStruct((2, 4 * PART, WIDE), F32),
            jax.ShapeDtypeStruct((24, 128), F32),
        ],
        in_specs=[smem] * 2 + [vmem] * 12 + [hbm] * 4,
        out_specs=[hbm, hbm, vmem, vmem, vmem],
        scratch_shapes=[
            packed(strips, row_count, width),
            packed(strips, row_count, width),
            packed(strips, row_count, width),
            wide(rows, width),
            packed(rows, width),
            packed(rows, 3 * width),
            packed(rows, width),
            wide(rows, 128),
            wide(rows, width),
            packed(rows, width),
            packed(rows, width),
            wide(rows, width),
            wide(rows, width),
            packed(rows, width),
            packed(rows, width),
            packed(rows, width),
            packed(rows, width),
            packed(width, width),
            wide(8, width),
            wide(8, width),
            wide(8, width),
            wide(8, width),
            packed(width, 3 * width),
            packed(width, width),
            packed(2, width, width),
            packed(2, width, width),
            packed(2 * SLOTS, 2, 384, WIDE),
            packed(CHUNKS, 384, WIDE),
            packed(CHUNKS, 192, WIDE),
            packed(CHUNKS, 96, WIDE),
            packed(OWN, 48, WIDE),
            packed(OWN, 2, 24, WIDE),
            packed(OWN, 24, WIDE),
            packed(CHUNKS - OWN, 96, WIDE),
            packed(CHUNKS - OWN, 96, WIDE),
        ]
        + [wide(7, 8, width)] * 2
        + [
            pltpu.SemaphoreType.DMA((STAGES, CHUNKS)),
            pltpu.SemaphoreType.DMA((STAGES, CHUNKS)),
            pltpu.SemaphoreType.DMA((2, 7)),
            pltpu.SemaphoreType.DMA((2, 7)),
            pltpu.SemaphoreType.DMA((4, strips)),
            pltpu.SemaphoreType.DMA((4, strips)),
            pltpu.SemaphoreType.DMA((2,)),
            pltpu.SemaphoreType.DMA((2, 2)),
            pltpu.SemaphoreType.DMA((4,)),
        ],
        compiler_params=pltpu.CompilerParams(
            collective_id=0, has_side_effects=True, vmem_limit_bytes=67043328
        ),
    )(*arrays)


def finish_kernel(
    layer_in, grad_in, reduced, reduced_down, small,
    layer_out, grad_patches, table, gain_one, bias_one, qkv, query_bias, value_bias, out_weight,
    out_bias, gain_two, bias_two, up_weight, up_bias, down_weight, down_bias,
):
    for j in range(layer_in.shape[0]):
        layer_out[:, j, :] = layer_in[j]
        grad_patches[:, j, :] = grad_in[j]
    names = {
        0: gain_two, 1: bias_two, 2: out_bias, 3: down_bias,
        8: gain_one, 9: bias_one, 10: query_bias, 11: value_bias,
    }
    for index, ref in names.items():
        ref[...] = small[pl.ds(index, 1), pl.ds(0, PART)].reshape(PART)
    up_bias[...] = column_sum(small[pl.ds(16, 8), pl.ds(0, 4 * PART)]).reshape(4 * PART)
    table[...] = small[pl.ds(12, 4), pl.ds(0, PART)]
    for c in range(8):
        up_weight[:, pl.ds(c * WIDE, WIDE)] = reduced[c]
    for c in range(2):
        out_weight[:, pl.ds(c * WIDE, WIDE)] = reduced[8 + c]
    for half in range(2):
        down_weight[:, pl.ds(half * WIDE, WIDE)] = reduced_down[half]
    width = qkv.shape[1] // 3
    for pair in range(6):
        for part in range(3):
            qkv[:, pl.ds(part * width + pair * 128, 128)] = reduced[
                10 + pair, :, pl.ds(part * 128, 128)
            ]


def local(
    patches,
    lengths,
    script,
    script_table,
    gain_one,
    bias_one,
    qkv_weight,
    query_bias,
    value_bias,
    out_weight,
    out_bias,
    gain_two,
    bias_two,
    up_weight,
    up_bias,
    down_weight,
    down_bias,
    cotangent,
):
    strips, row_count, width = patches.shape
    groups = script_table.shape[0]
    results = run_layer(
        lengths, script, script_table, gain_one, bias_one, query_bias, value_bias, out_bias,
        gain_two, bias_two, up_bias, down_bias, patches.transpose(1, 0, 2),
        cotangent.transpose(1, 0, 2), qkv_weight,
        out_weight, up_weight, down_weight,
    )
    vector = jax.ShapeDtypeStruct((PART,), F32)
    turned = jax.ShapeDtypeStruct((row_count, strips, width), BF)
    outputs = pl.pallas_call(
        finish_kernel,
        out_shape=[
            turned,
            turned,
            jax.ShapeDtypeStruct((groups, PART), F32),
            vector,
            vector,
            jax.ShapeDtypeStruct((PART, 3 * width), F32),
            vector,
            vector,
            jax.ShapeDtypeStruct((PART, width), F32),
            vector,
            vector,
            vector,
            jax.ShapeDtypeStruct((PART, up_weight.shape[1]), F32),
            jax.ShapeDtypeStruct((4 * PART,), F32),
            jax.ShapeDtypeStruct((4 * PART, width), F32),
            vector,
        ],
    )(*results)
    return (
        outputs[0].transpose(1, 0, 2),
        outputs[1].transpose(1, 0, 2),
        outputs[2].T,
        *outputs[3:],
    )


def solution(mesh):
    placed = (
        P("strip", "seq", None),
        P("strip"),
        P("strip"),
        P(),
        P(),
        P(),
        P(),
        P(),
        P(),
        P(),
        P(),
        P(),
        P(),
        P(),
        P(),
        P(),
        P(),
        P("strip", "seq", None),
    )
    chosen = local if fits(mesh) else local_general
    return jax.shard_map(
        chosen,
        mesh=mesh,
        in_specs=placed,
        out_specs=(
            P("strip", "seq", None),
            P("strip", "seq", None),
            P(("strip", "seq"), None),
            P(("strip", "seq")),
            P(("strip", "seq")),
            P(("strip", "seq"), None),
            P(("strip", "seq")),
            P(("strip", "seq")),
            P(("strip", "seq"), None),
            P(("strip", "seq")),
            P(("strip", "seq")),
            P(("strip", "seq")),
            P(("strip", "seq"), None),
            P(("strip", "seq")),
            P(("strip", "seq"), None),
            P(("strip", "seq")),
        ),
        check_vma=False,
    )
```

profile of v0, /device:TPU:0, one launch (start us, length us, event | category | flops | bytes accessed | tf_op | source)
XLA Modules:
  0.0 134.7 jit_solution(11064348781575653701)
XLA Ops:
  0.7 129.7 %shard_map.297 = (bf16[4,134,768]{2,1,0:T(8,128)(2,1)}, bf16[4,134,768]{2,1,0:T(8,128)(2,1)}, f32[16,24,384]{2,1,0:T(8,128)}, f32[2,96,384]{2,1,0:T(8,128)}, f32[24,128]{1,0:T(8,128)}) custom-call(s32[4]{0:T(128)} %lengths.1, s32[4]{0:T(128)} %script.1, bf16[4,768]{1,0:T(4,128)(2,1)} %table.1, f32[768]{0:T(1024)} %gain_one.1, f32[768]{0:T(1024)} %bias_one.1, ...), custom_call_target="tpu_custom_call" | custom-call | tf_op jit(solution)/shard_map/pallas_call | solution.py:1008
  130.4 4.1 %shard_map.298 = (bf16[134,4,768]{2,1,0:T(4,128)(2,1)}, bf16[134,4,768]{2,1,0:T(4,128)(2,1)}, f32[4,24]{1,0:T(4,128)}, f32[24]{0:T(128)}, f32[24]{0:T(128)}, /*i...) custom-call(bf16[4,134,768]{2,1,0:T(8,128)(2,1)} %get-tuple-element., ...), custom_call_target="tpu_custom_call" | custom-call | tf_op jit(solution)/shard_map/pallas_call | solution.py:1134
where the time goes:
time: 135 us
  Pallas kernels  134 us (99%)
    pallas_call x1, Pallas kernels, run_layer(): pl.pallas_call(layer_kernel, out_shape=[jax.ShapeDtypeStruct((strips, row...  130 us
    pallas_call x1, Pallas kernels, local(): pl.pallas_call(finish_kernel, out_shape=[turned, turned, jax.ShapeDtypeSt...  4.09 us

commit v1 on v0

--- a/solution.py
+++ b/solution.py
@@ -228,79 +228,70 @@
         [
             (0, 0, 0, 0, 0, 0, 0, 0, 0, 0, 0, 0, 0, 0, 0, 0, 0, 0, 0, 0),
             (0, 0, 0, 0, 0, 0, 0, 0, 0, 0, 2, 0, 0, 0, 0, 2, 0, 0, 0, 0),
-            (2, 0, 0, 0, 0, 2, 0, 0, 0, 0, 4, 0, 0, 0, 0, 4, 0, 0, 0, 0),
-            (4, 2, 0, 0, 0, 4, 1, 0, 0, 0, 6, 4, 0, 0, 0, 6, 3, 0, 0, 0),
-        ],
-        [
-            (0, 0, 0, 0, 0, 0, 0, 0, 0, 0, 0, 0, 0, 0, 0, 0, 0, 0, 0, 0),
-            (2, 0, 0, 0, 0, 2, 0, 0, 0, 0, 2, 0, 0, 0, 0, 2, 0, 0, 0, 0),
-            (4, 0, 0, 0, 0, 4, 0, 0, 0, 0, 4, 2, 0, 0, 0, 4, 1, 0, 0, 0),
-            (6, 4, 0, 0, 0, 6, 3, 0, 0, 0, 6, 4, 1, 0, 0, 6, 3, 0, 0, 0),
+            (2, 0, 0, 0, 0, 2, 0, 0, 0, 0, 4, 2, 0, 0, 0, 4, 1, 0, 0, 0),
+            (4, 2, 0, 0, 0, 4, 2, 0, 0, 0, 6, 2, 2, 0, 0, 6, 2, 1, 0, 0),
         ],
         [
             (0, 0, 0, 0, 0, 0, 0, 0, 0, 0, 0, 0, 0, 0, 0, 0, 0, 0, 0, 0),
             (2, 0, 0, 0, 0, 2, 0, 0, 0, 0, 2, 0, 0, 0, 0, 2, 0, 0, 0, 0),
             (4, 2, 0, 0, 0, 4, 1, 0, 0, 0, 4, 2, 0, 0, 0, 4, 1, 0, 0, 0),
-            (6, 4, 1, 0, 0, 6, 3, 0, 0, 0, 6, 4, 1, 0, 0, 6, 4, 0, 0, 0),
+            (6, 2, 2, 0, 0, 6, 2, 1, 0, 0, 6, 4, 2, 0, 0, 6, 2, 1, 0, 0),
+        ],
+        [
+            (0, 0, 0, 0, 0, 0, 0, 0, 0, 0, 0, 0, 0, 0, 0, 0, 0, 0, 0, 0),
+            (2, 0, 0, 0, 0, 2, 0, 0, 0, 0, 2, 0, 0, 0, 0, 2, 0, 0, 0, 0),
+            (4, 2, 0, 0, 0, 4, 1, 0, 0, 0, 4, 2, 0, 0, 0, 4, 2, 0, 0, 0),
+            (6, 4, 2, 0, 0, 6, 2, 1, 0, 0, 6, 4, 2, 0, 0, 6, 3, 1, 0, 0),
         ],
     ],
     "after": [
-        (6, 4, 1, 0, 0, 6, 4, 0, 0, 0, 8, 4, 3, 0, 0, 8, 4, 0, 0, 0),
-        (8, 4, 3, 0, 0, 8, 4, 0, 0, 0, 8, 4, 3, 0, 0, 8, 4, 2, 0, 0),
-        (8, 4, 3, 0, 0, 8, 4, 2, 0, 0, 8, 4, 4, 1, 0, 8, 4, 2, 0, 0),
+        (6, 4, 2, 0, 0, 6, 3, 1, 0, 0, 8, 4, 2, 2, 0, 7, 4, 2, 1, 0),
+        (8, 4, 2, 2, 0, 7, 4, 2, 1, 0, 8, 4, 2, 2, 0, 8, 5, 2, 1, 0),
+        (8, 4, 2, 2, 0, 8, 5, 2, 1, 0, 8, 6, 3, 2, 0, 8, 5, 2, 1, 0),
     ],
     "pair": [
-        (8, 4, 4, 1, 0, 8, 4, 2, 0, 0, 10, 4, 4, 1, 0, 8, 5, 3, 0, 0),
-        (10, 4, 4, 1, 0, 8, 5, 3, 0, 0, 10, 6, 4, 1, 0, 8, 5, 3, 0, 0),
-        (10, 6, 4, 1, 1, 8, 6, 3, 3, 0, 12, 8, 4, 1, 1, 8, 6, 3, 3, 0),
-        (12, 8, 4, 1, 1, 8, 6, 3, 3, 0, 12, 8, 4, 3, 1, 8, 6, 5, 3, 2),
-        (12, 10, 4, 4, 1, 8, 8, 5, 3, 3, 14, 10, 8, 4, 3, 8, 8, 6, 4, 3),
-        (14, 10, 8, 4, 3, 8, 8, 6, 4, 3, 14, 12, 9, 4, 4, 8, 8, 6, 5, 3),
+        (8, 6, 3, 2, 0, 8, 5, 2, 1, 0, 10, 6, 4, 2, 2, 8, 6, 2, 2, 1),
+        (10, 6, 4, 2, 2, 8, 6, 2, 2, 1, 10, 6, 4, 3, 2, 8, 6, 3, 2, 1),
+        (10, 8, 4, 3, 2, 8, 6, 3, 2, 2, 12, 8, 4, 3, 3, 8, 6, 5, 3, 2),
+        (12, 8, 4, 3, 3, 8, 6, 5, 3, 2, 12, 10, 4, 4, 3, 8, 8, 5, 3, 2),
+        (12, 10, 6, 4, 3, 8, 8, 5, 5, 3, 14, 12, 7, 4, 3, 8, 8, 7, 5, 3),
+        (14, 12, 7, 4, 3, 8, 8, 7, 5, 3, 14, 12, 9, 7, 4, 8, 8, 7, 5, 4),
     ],
     "grad": [
         [
-            (10, 6, 4, 1, 0, 8, 5, 3, 0, 0, 10, 6, 4, 1, 0, 8, 6, 3, 2, 0),
-            (12, 8, 4, 3, 1, 8, 6, 5, 3, 2, 12, 8, 4, 4, 1, 8, 8, 5, 3, 3),
-            (14, 12, 9, 4, 4, 8, 8, 6, 5, 3, 14, 12, 9, 6, 4, 8, 8, 8, 5, 3),
+            (10, 6, 4, 3, 2, 8, 6, 3, 2, 1, 10, 8, 4, 3, 2, 8, 6, 3, 2, 1),
+            (12, 10, 4, 4, 3, 8, 8, 5, 3, 2, 12, 10, 5, 4, 3, 8, 8, 5, 3, 2),
+            (14, 12, 9, 7, 4, 8, 8, 7, 5, 4, 14, 12, 10, 7, 4, 8, 8, 7, 6, 5),
         ],
         [
-            (10, 6, 4, 1, 0, 8, 6, 3, 2, 0, 10, 6, 4, 1, 1, 8, 6, 3, 3, 0),
-            (12, 8, 4, 4, 1, 8, 8, 5, 3, 3, 12, 10, 4, 4, 1, 8, 8, 5, 3, 3),
-            (14, 12, 9, 6, 4, 8, 8, 8, 5, 3, 14, 12, 10, 8, 4, 8, 8, 8, 5, 4),
+            (10, 8, 4, 3, 2, 8, 6, 3, 2, 1, 10, 8, 4, 3, 2, 8, 6, 3, 2, 2),
+            (12, 10, 5, 4, 3, 8, 8, 5, 3, 2, 12, 10, 6, 4, 3, 8, 8, 5, 5, 3),
+            (14, 12, 10, 7, 4, 8, 8, 7, 6, 5, 14, 13, 10, 7, 4, 8, 8, 8, 7, 5),
         ],
     ],
     "last": [
-        (14, 12, 10, 8, 4, 8, 8, 8, 5, 4, 16, 13, 11, 8, 4, 8, 8, 8, 6, 4),
-        (16, 13, 11, 8, 4, 8, 8, 8, 6, 4, 16, 14, 11, 8, 4, 8, 8, 8, 6, 4),
+        (14, 13, 10, 7, 4, 8, 8, 8, 7, 5, 16, 14, 11, 8, 4, 8, 8, 8, 7, 5),
+        (16, 14, 11, 8, 4, 8, 8, 8, 7, 5, 16, 14, 12, 8, 5, 8, 8, 8, 7, 5),
     ],
     "tail": [
-        (16, 14, 11, 8, 4, 8, 8, 8, 6, 4, 16, 14, 12, 8, 4, 8, 8, 8, 6, 4),
-        (16, 14, 12, 8, 4, 8, 8, 8, 6, 4, 16, 14, 12, 10, 4, 8, 8, 8, 6, 4),
-        (16, 14, 12, 10, 4, 8, 8, 8, 6, 4, 16, 14, 12, 10, 4, 8, 8, 8, 6, 5),
-        (16, 14, 12, 10, 4, 8, 8, 8, 6, 5, 16, 14, 12, 10, 5, 8, 8, 8, 6, 5),
-        (16, 14, 12, 10, 5, 8, 8, 8, 6, 5, 16, 14, 12, 10, 6, 8, 8, 8, 6, 5),
-        (16, 14, 12, 10, 6, 8, 8, 8, 6, 5, 16, 14, 12, 10, 6, 8, 8, 8, 7, 5),
-        (16, 14, 12, 10, 6, 8, 8, 8, 7, 5, 16, 14, 13, 10, 6, 8, 8, 8, 7, 5),
-        (16, 14, 13, 10, 6, 8, 8, 8, 7, 5, 16, 14, 13, 10, 6, 8, 8, 8, 8, 5),
-        (16, 14, 13, 10, 6, 8, 8, 8, 8, 5, 16, 14, 13, 10, 7, 8, 8, 8, 8, 5),
-        (16, 14, 13, 10, 7, 8, 8, 8, 8, 5, 16, 14, 13, 10, 8, 8, 8, 8, 8, 5),
-        (16, 14, 13, 10, 8, 8, 8, 8, 8, 5, 16, 15, 13, 10, 8, 8, 8, 8, 8, 5),
-        (16, 15, 13, 10, 8, 8, 8, 8, 8, 5, 16, 15, 13, 11, 8, 8, 8, 8, 8, 5),
-        (16, 15, 13, 11, 8, 8, 8, 8, 8, 5, 16, 15, 13, 11, 8, 8, 8, 8, 8, 6),
-        (16, 15, 13, 11, 8, 8, 8, 8, 8, 6, 16, 15, 14, 11, 8, 8, 8, 8, 8, 6),
-        (16, 15, 14, 11, 8, 8, 8, 8, 8, 6, 16, 16, 14, 11, 8, 8, 8, 8, 8, 6),
-        (16, 16, 14, 11, 8, 8, 8, 8, 8, 6, 16, 16, 14, 11, 9, 8, 8, 8, 8, 6),
-        (16, 16, 14, 11, 9, 8, 8, 8, 8, 6, 16, 16, 14, 11, 10, 8, 8, 8, 8, 6),
-        (16, 16, 14, 11, 10, 8, 8, 8, 8, 6, 16, 16, 14, 13, 10, 8, 8, 8, 8, 6),
-        (16, 16, 14, 13, 10, 8, 8, 8, 8, 6, 16, 16, 14, 13, 10, 8, 8, 8, 8, 7),
-        (16, 16, 14, 13, 10, 8, 8, 8, 8, 7, 16, 16, 15, 13, 10, 8, 8, 8, 8, 7),
-        (16, 16, 15, 13, 10, 8, 8, 8, 8, 7, 16, 16, 15, 14, 11, 8, 8, 8, 8, 7),
-        (16, 16, 15, 14, 11, 8, 8, 8, 8, 7, 16, 16, 16, 14, 11, 8, 8, 8, 8, 8),
-        (16, 16, 16, 14, 11, 8, 8, 8, 8, 8, 16, 16, 16, 14, 12, 8, 8, 8, 8, 8),
+        (16, 14, 12, 8, 5, 8, 8, 8, 7, 5, 16, 14, 12, 10, 7, 8, 8, 8, 7, 5),
+        (16, 14, 12, 10, 7, 8, 8, 8, 7, 5, 16, 14, 13, 10, 7, 8, 8, 8, 7, 5),
+        (16, 14, 13, 10, 7, 8, 8, 8, 7, 5, 16, 14, 13, 10, 7, 8, 8, 8, 7, 6),
+        (16, 14, 13, 10, 7, 8, 8, 8, 7, 6, 16, 14, 14, 10, 7, 8, 8, 8, 8, 6),
+        (16, 14, 14, 10, 7, 8, 8, 8, 8, 6, 16, 14, 14, 11, 7, 8, 8, 8, 8, 7),
+        (16, 14, 14, 11, 7, 8, 8, 8, 8, 7, 16, 14, 14, 11, 8, 8, 8, 8, 8, 7),
+        (16, 14, 14, 11, 8, 8, 8, 8, 8, 7, 16, 15, 14, 11, 8, 8, 8, 8, 8, 7),
+        (16, 15, 14, 11, 8, 8, 8, 8, 8, 7, 16, 15, 14, 12, 8, 8, 8, 8, 8, 7),
+        (16, 15, 14, 12, 8, 8, 8, 8, 8, 7, 16, 16, 14, 12, 8, 8, 8, 8, 8, 7),
+        (16, 16, 14, 12, 8, 8, 8, 8, 8, 7, 16, 16, 14, 12, 9, 8, 8, 8, 8, 7),
+        (16, 16, 14, 12, 9, 8, 8, 8, 8, 7, 16, 16, 14, 14, 9, 8, 8, 8, 8, 7),
+        (16, 16, 14, 14, 9, 8, 8, 8, 8, 7, 16, 16, 14, 14, 10, 8, 8, 8, 8, 7),
+        (16, 16, 14, 14, 10, 8, 8, 8, 8, 7, 16, 16, 15, 14, 10, 8, 8, 8, 8, 7),
+        (16, 16, 15, 14, 10, 8, 8, 8, 8, 7, 16, 16, 15, 14, 11, 8, 8, 8, 8, 7),
+        (16, 16, 15, 14, 11, 8, 8, 8, 8, 7, 16, 16, 16, 14, 12, 8, 8, 8, 8, 8),
         (16, 16, 16, 14, 12, 8, 8, 8, 8, 8, 16, 16, 16, 14, 13, 8, 8, 8, 8, 8),
-        (16, 16, 16, 14, 13, 8, 8, 8, 8, 8, 16, 16, 16, 15, 13, 8, 8, 8, 8, 8),
-        (16, 16, 16, 15, 13, 8, 8, 8, 8, 8, 16, 16, 16, 16, 13, 8, 8, 8, 8, 8),
-        (16, 16, 16, 16, 13, 8, 8, 8, 8, 8, 16, 16, 16, 16, 14, 8, 8, 8, 8, 8),
+        (16, 16, 16, 14, 13, 8, 8, 8, 8, 8, 16, 16, 16, 15, 14, 8, 8, 8, 8, 8),
+        (16, 16, 16, 15, 14, 8, 8, 8, 8, 8, 16, 16, 16, 16, 14, 8, 8, 8, 8, 8),
         (16, 16, 16, 16, 14, 8, 8, 8, 8, 8, 16, 16, 16, 16, 15, 8, 8, 8, 8, 8),
         (16, 16, 16, 16, 15, 8, 8, 8, 8, 8, 16, 16, 16, 16, 16, 8, 8, 8, 8, 8),
     ],
@@ -325,9 +316,9 @@
     return jnp.sum(block.reshape(block.shape[0] // 8, 8, block.shape[1]), axis=0)
 
 
-def sweep(blocks, body, totals):
-    def trip(first, size, totals):
-        results = [body(first + k) for k in range(size)]
+def sweep(blocks, body, totals, first=0):
+    def trip(start, size, totals):
+        results = [body(start + k) for k in range(size)]
         for stores, _ in results:
             for ref, at, value in stores:
                 ref[at] = value
@@ -335,9 +326,10 @@
             total + sum(sums[k] for _, sums in results) for k, total in enumerate(totals)
         )
 
-    totals = lax.fori_loop(0, blocks // 4, lambda i, t: trip(4 * i, 4, t), totals)
-    if blocks % 4:
-        totals = trip(blocks // 4 * 4, blocks % 4, totals)
+    whole = (blocks - first) // 4
+    totals = lax.fori_loop(0, whole, lambda i, t: trip(first + 4 * i, 4, t), totals)
+    if (blocks - first) % 4:
+        totals = trip(first + 4 * whole, (blocks - first) % 4, totals)
     return totals
 
 
@@ -351,12 +343,10 @@
     return jnp.sum(block, axis=0, keepdims=True)
 
 
-def attend_pair(pair, length, proj, mixed, lse_all):
-    count = proj.shape[0]
+def attend_pair(pair, visible, proj, mixed, lse_all):
     width = proj.shape[1] // 3
     at = lambda part: pl.ds(pl.multiple_of(part * width + pair * 128, 128), 128)
     lane = lax.broadcasted_iota(jnp.int32, (1, 128), 1)
-    visible = lax.broadcasted_iota(jnp.int32, (1, count), 1) < length
     q = proj[:, at(0)] * jnp.asarray(0.125, BF)
     k = proj[:, at(1)]
     v = proj[:, at(2)]
@@ -376,12 +366,10 @@
     lse_all[...] = jnp.where(lane == 2 * pair + 1, logs[1], known)
 
 
-def attend_pair_back(pair, length, proj, gmixed, lse_all):
-    count = proj.shape[0]
+def attend_pair_back(pair, visible, proj, gmixed, lse_all):
     width = proj.shape[1] // 3
     at = lambda part: pl.ds(pl.multiple_of(part * width + pair * 128, 128), 128)
     lane = lax.broadcasted_iota(jnp.int32, (1, 128), 1)
-    visible = lax.broadcasted_iota(jnp.int32, (1, count), 1) < length
     q = proj[:, at(0)] * jnp.asarray(0.125, BF)
     k = proj[:, at(1)]
     v = proj[:, at(2)]
@@ -450,7 +438,7 @@
         if down:
             by_x, by_y, by_low = ((odd, even, 0), (even, odd, 0), (0, 0, 1))[stage - 1]
         else:
-            by_x, by_y, by_low = ((even, 0, odd), (odd, even, 0), (0, odd, even))[stage - 1]
+            by_x, by_y, by_low = ((even, 0, odd), (0, 1, 0), (odd, 0, even))[stage - 1]
         device = (
             dev.s + by_x * (1 - 2 * dev.x) + by_low * (2 - 4 * dev.low),
             dev.q + by_y * (2 - 4 * dev.y),
@@ -515,19 +503,17 @@
         if stage == 0:
             slot = self.slot(c, down)
 
-            @pl.loop(0, 4)
+            @pl.loop(0, 2)
             def _(i):
-                rows = pl.ds(i * 96, 96)
+                rows = pl.ds(pl.multiple_of(i * 192, 192), 192)
                 r1[c, rows] = r1[c, rows] + g[slot, dev.core, rows]
         elif stage < 3:
             _, bit = self.side(stage, c, down)
             held, target = ((r1, r2), (r2, r3))[stage - 1]
 
-            @pl.loop(0, 4 >> stage)
-            def _(i):
-                rows = pl.ds(i * 96, 96)
-                kept = pl.ds(pl.multiple_of(bit * (384 >> stage) + i * 96, 96), 96)
-                target[c, rows] = target[c, rows] + held[c, kept]
+            size = 384 >> stage
+            kept = pl.ds(pl.multiple_of(bit * size, size), size)
+            target[c] = target[c] + held[c, kept]
         elif stage == 3:
             _, bit = self.side(stage, c, down)
             kept = pl.ds(pl.multiple_of(bit * 48, 48), 48)
@@ -606,7 +592,7 @@
         columns = pl.ds(half * WIDE, WIDE)
         for owner in range(32):
             core, y, x, low, high = [(owner >> bit) % 2 for bit in range(5)]
-            unit = 4 * low + 2 * x + y if half else 4 * x + 2 * y + low
+            unit = 4 * low + 2 * y + x if half else 4 * x + 2 * y + low
             self.bufs[0][self.slot(c, False), core, pl.ds(unit * 48 + high * PART, PART)] = product[
                 pl.ds(owner * PART, PART), columns
             ]
@@ -687,15 +673,15 @@
         )
 
     def exchange(group, source, target):
+        near, across = q + 1 - 2 * dev.core, q + 2 - 4 * dev.y
         copies = []
-        for hop in range(1, strips):
-            other = (q + hop) % strips
+        for k, other in enumerate((near, across, near + 2 - 4 * dev.y)):
             copies.append(
                 pltpu.make_async_remote_copy(
                     src_ref=source.at[other],
                     dst_ref=target.at[q],
-                    send_sem=xsend.at[group, hop],
-                    recv_sem=xrecv.at[group, hop],
+                    send_sem=xsend.at[group, k],
+                    recv_sem=xrecv.at[group, k],
                     device_id=(s, other),
                     device_id_type=MESH,
                 )
@@ -705,9 +691,17 @@
 
     def launch(moves):
         copies, own = moves
-        for index in (1, 0, 2):
+        for index in (1, 2, 0):
             copies[index].start()
         own.start()
+
+    def order(m):
+        return (2 * dev.y + m) % strips
+
+    def seen():
+        local = lax.broadcasted_iota(jnp.int32, (1, rows), 1)
+        shift = jnp.where(local < count // 2, count // 2, -(count // 2)) * dev.y
+        return (local + shift < length) & (local < count)
 
     def arrive(moves):
         copies, own = moves
@@ -785,35 +779,45 @@
     for block in range(ff_blocks):
         ubias[pl.ds(block, 1)] = row(up_bias)[:, block * width : block * width + width]
 
-    arrive(into_x)
+    def first_norm(b):
+        at = block_rows(b)
+        normed, _ = standardize(hidden[at])
+        return [(n1, at, (normed * row(gain_one) + row(bias_one)).astype(BF))], ()
+
+    def project(first, size):
+        @pl.loop(0, 3)
+        def _(part):
+            columns = pl.ds(pl.multiple_of(part * width, width), width)
+            made = dot(n1[pl.ds(first, size)], wqkv[:, columns], 1, 0) + jbias[pl.ds(part, 1)]
+            proj[pl.ds(first, size), columns] = made.astype(BF)
+
+    into_x[0][0].wait_recv()
+    into_x[1].wait()
+    for m in range(2):
+        hidden[pl.ds(m * row_count, row_count)] = xin[order(m)].astype(F32) + added
+    early_rows = 2 * row_count // (4 * BLOCK) * (4 * BLOCK)
+    sweep(early_rows // BLOCK, first_norm, ())
+    load_qkv.wait()
+    project(0, early_rows)
+
+    for copy in into_x[0][1:]:
+        copy.wait_recv()
     sent(into_x)
     for j in range(strips):
         outgoing[j] = cotangent[:, j, :]
     launch(into_c)
-    for j in range(strips):
-        hidden[pl.ds(j * row_count, row_count)] = xin[j].astype(F32) + added
-
-    def first_norm(b):
-        at = block_rows(b)
-        normed, _ = standardize(hidden[at])
-        return [(n1, at, (normed * row(gain_one) + row(bias_one)).astype(BF))], ()
-
-    sweep(blocks, first_norm, ())
-
-    load_qkv.wait()
-
-    @pl.loop(0, 3)
-    def _(part):
-        columns = pl.ds(pl.multiple_of(part * width, width), width)
-        proj[:, columns] = (dot(n1[...], wqkv[:, columns], 1, 0) + jbias[pl.ds(part, 1)]).astype(BF)
+    for m in range(2, strips):
+        hidden[pl.ds(m * row_count, row_count)] = xin[order(m)].astype(F32) + added
+    sweep(blocks, first_norm, (), early_rows // BLOCK)
+    project(early_rows, rows - early_rows)
 
     @pl.loop(0, width // 128)
     def _(pair):
-        attend_pair(pair, length, proj, mixed, lse_all)
+        attend_pair(pair, seen(), proj, mixed, lse_all)
 
     arrive(into_c)
     for j in range(strips):
-        gn[pl.ds(j * row_count, row_count)] = cin[j].astype(F32)
+        gn[pl.ds(j * row_count, row_count)] = cin[order(j)].astype(F32)
     load_out.wait()
     att[...] = hidden[...] + dot(mixed[...], wout[...], 1, 0) + row(out_bias)
     zero8 = jnp.zeros((8, width), F32)
@@ -874,7 +878,7 @@
 
     sent(into_c)
     for j in range(strips):
-        outgoing[j] = res[pl.ds(j * row_count, row_count)].astype(BF)
+        outgoing[order(j)] = res[pl.ds(j * row_count, row_count)].astype(BF)
     from_out = exchange(2, outgoing, layer_out)
     launch(from_out)
 
@@ -913,7 +917,7 @@
         @pl.loop(0, 2)
         def _(h):
             pair = 2 * i + h
-            grads = attend_pair_back(pair, length, proj, gmixed, lse_all)
+            grads = attend_pair_back(pair, seen(), proj, gmixed, lse_all)
             for part in range(3):
                 gblk[:, pl.ds(pl.multiple_of(h * WIDE + part * 128, 128), 128)] = grads[part]
             lanes = pl.ds(pl.multiple_of(pair * 128, 128), 128)
@@ -963,14 +967,17 @@
     share_late = share(1, late, late_in)
     share_late[0](0)
     for j in range(strips):
-        xin[j] = res[pl.ds(j * row_count, row_count)].astype(BF)
+        xin[order(j)] = res[pl.ds(j * row_count, row_count)].astype(BF)
     from_grad = exchange(3, xin, grad_patches)
-    launch(from_grad)
     red.step(PLAN["last"][1:])
     tail = PLAN["tail"]
     turns = [len(tail) * (turn + 1) // 4 for turn in range(3)]
+    waiting = True
     for index in range(len(tail)):
         red.step(tail[index : index + 1])
+        if waiting and tail[index][2 * STAGES + 1] == OWN:
+            launch(from_grad)
+            waiting = False
         for turn in range(3):
             if turns[turn] == index:
                 share_late[1](turn)

time: 135 us -> 131 us (0.970)
  Pallas kernels: 134 us -> 130 us
    pallas_call x1, Pallas kernels: 130 us -> 126 us  [run_layer(): pl.pallas_call(layer_kernel, out_shape=[jax.ShapeDtypeStruct((strips, row...]
where the time goes in v1:
time: 131 us; the launch traced here: 130 us
  Pallas kernels  130 us (99%)
    pallas_call x1, Pallas kernels, run_layer(): pl.pallas_call(layer_kernel, out_shape=[jax.ShapeDtypeStruct((strips, row...  126 us
    pallas_call x1, Pallas kernels, local(): pl.pallas_call(finish_kernel, out_shape=[turned, turned, jax.ShapeDtypeSt...  4.09 us

profile of v1, /device:TPU:0, one launch (start us, length us, event | category | flops | bytes accessed | tf_op | source)
XLA Modules:
  0.0 130.4 jit_solution(4131265203431791936)
XLA Ops:
  0.7 125.5 %shard_map.297 = (bf16[4,134,768]{2,1,0:T(8,128)(2,1)}, bf16[4,134,768]{2,1,0:T(8,128)(2,1)}, f32[16,24,384]{2,1,0:T(8,128)}, f32[2,96,384]{2,1,0:T(8,128)}, f32[24,128]{1,0:T(8,128)}) custom-call(s32[4]{0:T(128)} %lengths.1, s32[4]{0:T(128)} %script.1, bf16[4,768]{1,0:T(4,128)(2,1)} %table.1, f32[768]{0:T(1024)} %gain_one.1, f32[768]{0:T(1024)} %bias_one.1, ...), custom_call_target="tpu_custom_call" | custom-call | tf_op jit(solution)/shard_map/pallas_call | solution.py:1015
  126.2 4.1 %shard_map.298 = (bf16[134,4,768]{2,1,0:T(4,128)(2,1)}, bf16[134,4,768]{2,1,0:T(4,128)(2,1)}, f32[4,24]{1,0:T(4,128)}, f32[24]{0:T(128)}, f32[24]{0:T(128)}, /*i...) custom-call(bf16[4,134,768]{2,1,0:T(8,128)(2,1)} %get-tuple-element., ...), custom_call_target="tpu_custom_call" | custom-call | tf_op jit(solution)/shard_map/pallas_call | solution.py:1141
